TPU v7x, 32 devices: a whole 2x2x4 slice. The times are simulated.
32 devices in a mesh: rep: 2 (over y), shard: 16 (over z, x, core).
Axes of the slice: x: 2, y: 2, z: 4, core: 2. Of those that a mesh axis runs over, the one named last changes fastest.
Arguments:
- tokens: bfloat16 [2, 3072, 768], P('rep', 'shard'), may hold values from -6 to 6
- segments: int32 [2, 3072], P('rep', 'shard'), may hold values from 0 to 16, never falling along the last dimension, each value on 1 to 2304 neighbouring positions
- padding: int32 [2, 3072], P('rep', 'shard'), may hold values from 0 to 1, as said below
- query_weight: float32 [768, 768], P('shard'), may hold values from -0.21875 to 0.21875
- key_weight: float32 [768, 768], P('shard'), may hold values from -0.21875 to 0.21875
- value_weight: float32 [768, 768], P('shard'), may hold values from -0.21875 to 0.21875
- query_bias: float32 [768], P('shard'), may hold values from -3 to 3
- value_bias: float32 [768], P('shard'), may hold values from -3 to 3
- out_weight: float32 [768, 768], P('shard'), may hold values from -0.875 to 0.875
- out_bias: float32 [768], P('shard'), may hold values from -3 to 3
- middle_gain: float32 [768], P('shard'), may hold values from 0.5 to 1.5
- middle_shift: float32 [768], P('shard'), may hold values from -3 to 3
- up_weight: float32 [768, 3072], P('shard'), may hold values from -0.21875 to 0.21875
- up_bias: float32 [3072], P('shard'), may hold values from -3 to 3
- down_weight: float32 [3072, 768], P('shard'), may hold values from -0.109375 to 0.109375
- down_bias: float32 [768], P('shard'), may hold values from -3 to 3
- final_gain: float32 [768], P('shard'), may hold values from 0.5 to 1.5
- final_shift: float32 [768], P('shard'), may hold values from -3 to 3
- cotangent: bfloat16 [2, 3072, 768], P('rep', 'shard'), may hold values from -6 to 6
Outputs:
- output: bfloat16 [2, 3072, 768], P('rep', 'shard')
- grad_tokens: bfloat16 [2, 3072, 768], P('rep', 'shard')
- grad_query_weight: float32 [768, 768], P('shard')
- grad_key_weight: float32 [768, 768], P('shard')
- grad_value_weight: float32 [768, 768], P('shard')
- grad_query_bias: float32 [768], P('shard')
- grad_value_bias: float32 [768], P('shard')
- grad_out_weight: float32 [768, 768], P('shard')
- grad_out_bias: float32 [768], P('shard')
- grad_middle_gain: float32 [768], P('shard')
- grad_middle_shift: float32 [768], P('shard')
- grad_up_weight: float32 [768, 3072], P('shard')
- grad_up_bias: float32 [3072], P('shard')
- grad_down_weight: float32 [3072, 768], P('shard')
- grad_down_bias: float32 [768], P('shard')
- grad_final_gain: float32 [768], P('shard')
- grad_final_shift: float32 [768], P('shard')
Inputs may be any that keep to these rules, and one draw needn't show every extreme that they name: `segments`: within each sequence the numbers never fall; every document has 1 to 2304 tokens and one has exactly 2304. Each sequence ends with a run of at least one padding token and has no other padding.
All inputs are finite; a program needn't handle non-finite values.
Results may differ from a plain program's by a relative error of at most 0.024.
Values may be sent and summed in bfloat16 or wider, within the bound.
A program may use at most 256 MiB of HBM per device.

v0:
```python
import jax
import jax.numpy as jnp
from jax import lax
from jax.sharding import PartitionSpec as P

D = 768
HEADS = 12
HEAD_DIM = 64
epsilon = 1e-12
very_low = -1e30
block_size = 512
root_half = 0.7071067811865476
inv_root_tau = 0.3989422804014327


def split_size():
    return block_size


def over_blocks(update, initial, arrays, total_rows):
    length = split_size()
    number = total_rows // length
    split = tuple((item.reshape((number, length) + item.shape[1:]) for item in arrays))

    def advance(carried, pieces):
        return (update(carried, pieces), None)

    return lax.scan(advance, initial, split)[0]


def scan_blocks(step, initial, arrays, total_rows):
    length = split_size()
    number = total_rows // length
    split = tuple((item.reshape((number, length) + item.shape[1:]) for item in arrays))
    final, produced = lax.scan(step, initial, split)
    return (final, produced.reshape((total_rows,) + produced.shape[2:]))


def guarded_update(update):

    def run_update(carried, pieces):
        return update(carried, pieces)

    return run_update


def guarded_step(step):

    def run_step(carried, pieces):
        return step(carried, pieces)

    return run_step


def norm_forward(value, gain, shift):
    center = value - jnp.mean(value, axis=-1, keepdims=True)
    spread = jnp.mean(center * center, axis=-1, keepdims=True)
    scale = lax.rsqrt(spread + epsilon)
    normal = center * scale
    return (normal * gain + shift, normal, scale)


def norm_backward(upstream, normal, scale, gain):
    inner = upstream * gain
    return scale * (
        inner
        - jnp.mean(inner, axis=-1, keepdims=True)
        - normal * jnp.mean(inner * normal, axis=-1, keepdims=True)
    )


def gelu_slope(hidden):
    return 0.5 * (1.0 + lax.erf(hidden * root_half)) + hidden * inv_root_tau * jnp.exp(
        -0.5 * hidden * hidden
    )


def score_grads(
    queries, query_codes, log_rows, delta_rows, dctx_rows, key_rows, value_rows, key_codes
):
    raw_scores = (
        jnp.einsum("qhd,khd->hqk", queries, key_rows, preferred_element_type=jnp.float32) * 0.125
    )
    allowed = (query_codes[:, None] == key_codes[None, :])[None]
    chances = jnp.where(allowed, jnp.exp(raw_scores - log_rows[:, :, None]), 0.0)
    d_chance = jnp.einsum("qhd,khd->hqk", dctx_rows, value_rows, preferred_element_type=jnp.float32)
    d_score = (chances * (d_chance - delta_rows[:, :, None])).astype(jnp.bfloat16)
    return (chances, d_score)


def forward_update(queries, codes_here):

    def update(carried, pieces):
        running_top, running_total, context_sum = carried
        key_rows, value_rows, key_codes = pieces
        raw_scores = (
            jnp.einsum("qhd,khd->hqk", queries, key_rows, preferred_element_type=jnp.float32)
            * 0.125
        )
        allowed = (codes_here[:, None] == key_codes[None, :])[None]
        masked = jnp.where(allowed, raw_scores, very_low)
        new_top = jnp.maximum(running_top, jnp.max(masked, axis=2))
        rescale = jnp.exp(running_top - new_top)
        weights = jnp.where(allowed, jnp.exp(masked - new_top[:, :, None]), 0.0)
        new_total = running_total * rescale + jnp.sum(weights, axis=2)
        added = jnp.einsum(
            "hqk,khd->qhd",
            weights.astype(jnp.bfloat16),
            value_rows,
            preferred_element_type=jnp.float32,
        )
        return (new_top, new_total, context_sum * rescale.T[:, :, None] + added)

    return guarded_update(update)


def shards(
    tokens,
    segments,
    padding,
    query_weight,
    key_weight,
    value_weight,
    query_bias,
    value_bias,
    out_weight,
    out_bias,
    middle_gain,
    middle_shift,
    up_weight,
    up_bias,
    down_weight,
    down_bias,
    final_gain,
    final_shift,
    cotangent,
):
    w_query, w_key, w_value, w_out, b_query, b_value, b_out, gain_mid, shift_mid = (
        lax.all_gather(query_weight.astype(jnp.bfloat16), "shard", axis=0, tiled=True),
        lax.all_gather(key_weight.astype(jnp.bfloat16), "shard", axis=0, tiled=True),
        lax.all_gather(value_weight.astype(jnp.bfloat16), "shard", axis=0, tiled=True),
        lax.all_gather(out_weight.astype(jnp.bfloat16), "shard", axis=0, tiled=True),
        lax.all_gather(query_bias.astype(jnp.bfloat16), "shard", axis=0, tiled=True),
        lax.all_gather(value_bias.astype(jnp.bfloat16), "shard", axis=0, tiled=True),
        lax.all_gather(out_bias.astype(jnp.bfloat16), "shard", axis=0, tiled=True),
        lax.all_gather(middle_gain.astype(jnp.bfloat16), "shard", axis=0, tiled=True),
        lax.all_gather(middle_shift.astype(jnp.bfloat16), "shard", axis=0, tiled=True),
    )
    w_up, b_up, w_down, b_down, gain_end, shift_end = (
        lax.all_gather(up_weight.astype(jnp.bfloat16), "shard", axis=0, tiled=True),
        lax.all_gather(up_bias.astype(jnp.bfloat16), "shard", axis=0, tiled=True),
        lax.all_gather(down_weight.astype(jnp.bfloat16), "shard", axis=0, tiled=True),
        lax.all_gather(down_bias.astype(jnp.bfloat16), "shard", axis=0, tiled=True),
        lax.all_gather(final_gain.astype(jnp.bfloat16), "shard", axis=0, tiled=True),
        lax.all_gather(final_shift.astype(jnp.bfloat16), "shard", axis=0, tiled=True),
    )
    own_tokens = tokens[0]
    here_rows = own_tokens.shape[0]
    own_codes = 2 * segments[0] + padding[0]
    all_codes = lax.all_gather(own_codes, "shard", axis=0, tiled=True)
    queries_flat = (
        jnp.dot(own_tokens, w_query, preferred_element_type=jnp.float32)
        + b_query.astype(jnp.float32)
    ).astype(jnp.bfloat16)
    keys_flat = jnp.dot(own_tokens, w_key, preferred_element_type=jnp.float32).astype(jnp.bfloat16)
    values_flat = (
        jnp.dot(own_tokens, w_value, preferred_element_type=jnp.float32)
        + b_value.astype(jnp.float32)
    ).astype(jnp.bfloat16)
    keys_all, values_all = (
        lax.all_gather(keys_flat, "shard", axis=0, tiled=True),
        lax.all_gather(values_flat, "shard", axis=0, tiled=True),
    )
    seq_rows = keys_all.shape[0]
    queries = queries_flat.reshape(here_rows, HEADS, HEAD_DIM)
    key_heads = keys_all.reshape(seq_rows, HEADS, HEAD_DIM)
    value_heads = values_all.reshape(seq_rows, HEADS, HEAD_DIM)
    start_state = (
        jnp.full((HEADS, here_rows), very_low, jnp.float32),
        jnp.zeros((HEADS, here_rows), jnp.float32),
        jnp.zeros((here_rows, HEADS, HEAD_DIM), jnp.float32),
    )
    best_score, total_weight, context_sum = over_blocks(
        forward_update(queries, own_codes),
        start_state,
        (key_heads, value_heads, all_codes),
        seq_rows,
    )
    log_total = best_score + jnp.log(total_weight)
    context = (context_sum / total_weight.T[:, :, None]).reshape(here_rows, D)
    context_low = context.astype(jnp.bfloat16)
    branch = jnp.dot(context_low, w_out, preferred_element_type=jnp.float32) + b_out.astype(
        jnp.float32
    )
    middle, normal_mid, scale_mid = norm_forward(
        own_tokens.astype(jnp.float32) + branch,
        gain_mid.astype(jnp.float32),
        shift_mid.astype(jnp.float32),
    )
    middle_low = middle.astype(jnp.bfloat16)
    hidden = jnp.dot(middle_low, w_up, preferred_element_type=jnp.float32) + b_up.astype(
        jnp.float32
    )
    active_low = jax.nn.gelu(hidden, approximate=False).astype(jnp.bfloat16)
    feed = jnp.dot(active_low, w_down, preferred_element_type=jnp.float32) + b_down.astype(
        jnp.float32
    )
    result, normal_end, scale_end = norm_forward(
        middle + feed, gain_end.astype(jnp.float32), shift_end.astype(jnp.float32)
    )
    output = result.astype(jnp.bfloat16)[None]
    upstream = cotangent[0].astype(jnp.float32)
    grad_gain_end = jnp.sum(upstream * normal_end, axis=0)
    grad_shift_end = jnp.sum(upstream, axis=0)
    d_second = norm_backward(upstream, normal_end, scale_end, gain_end.astype(jnp.float32))
    feed_low = d_second.astype(jnp.bfloat16)
    grad_down = lax.psum_scatter(
        jnp.einsum("tf,td->fd", active_low, feed_low, preferred_element_type=jnp.float32).astype(
            jnp.bfloat16
        ),
        "shard",
        scatter_dimension=0,
        tiled=True,
    )
    d_active = jnp.einsum("td,fd->tf", feed_low, w_down, preferred_element_type=jnp.float32)
    up_low = (d_active * gelu_slope(hidden)).astype(jnp.bfloat16)
    grad_up = lax.psum_scatter(
        jnp.einsum("td,tf->df", middle_low, up_low, preferred_element_type=jnp.float32).astype(
            jnp.bfloat16
        ),
        "shard",
        scatter_dimension=0,
        tiled=True,
    )
    d_middle = jnp.einsum("tf,df->td", up_low, w_up, preferred_element_type=jnp.float32) + d_second
    grad_gain_mid = jnp.sum(d_middle * normal_mid, axis=0)
    grad_shift_mid = jnp.sum(d_middle, axis=0)
    d_first = norm_backward(d_middle, normal_mid, scale_mid, gain_mid.astype(jnp.float32))
    branch_low = d_first.astype(jnp.bfloat16)
    dctx_low = jnp.einsum(
        "te,de->td", branch_low, w_out, preferred_element_type=jnp.float32
    ).astype(jnp.bfloat16)
    dctx_heads = dctx_low.reshape(here_rows, HEADS, HEAD_DIM)
    delta = jnp.sum(
        dctx_heads.astype(jnp.float32) * context.reshape(here_rows, HEADS, HEAD_DIM), axis=2
    ).T
    empty_heads = jnp.zeros((here_rows, HEADS, HEAD_DIM), jnp.float32)

    def key_step(carried, pieces):
        key_rows, value_rows, key_codes = pieces
        chances, d_score = score_grads(
            queries, own_codes, log_total, delta, dctx_heads, key_rows, value_rows, key_codes
        )
        block_rows = key_rows.shape[0]
        query_part = (
            carried
            + jnp.einsum("hqk,khd->qhd", d_score, key_rows, preferred_element_type=jnp.float32)
            * 0.125
        )
        d_key = (
            jnp.einsum("hqk,qhd->khd", d_score, queries, preferred_element_type=jnp.float32) * 0.125
        )
        d_value = jnp.einsum(
            "hqk,qhd->khd",
            chances.astype(jnp.bfloat16),
            dctx_heads,
            preferred_element_type=jnp.float32,
        )
        return (
            query_part,
            jnp.concatenate([d_key.reshape(block_rows, D), d_value.reshape(block_rows, D)], axis=1),
        )

    d_query, key_value_terms = scan_blocks(
        guarded_step(key_step), empty_heads, (key_heads, value_heads, all_codes), seq_rows
    )
    summed_kv = lax.psum_scatter(
        key_value_terms.astype(jnp.bfloat16), "shard", scatter_dimension=0, tiled=True
    ).astype(jnp.float32)
    key_grad = summed_kv[:, :D]
    value_grad = summed_kv[:, D:]
    query_low = d_query.reshape(here_rows, D).astype(jnp.bfloat16)
    key_low = key_grad.astype(jnp.bfloat16)
    value_low = value_grad.astype(jnp.bfloat16)
    mixer_part = lax.psum_scatter(
        jnp.concatenate(
            [
                jnp.einsum("td,te->de", own_tokens, query_low, preferred_element_type=jnp.float32),
                jnp.einsum("td,te->de", own_tokens, key_low, preferred_element_type=jnp.float32),
                jnp.einsum("td,te->de", own_tokens, value_low, preferred_element_type=jnp.float32),
                jnp.einsum(
                    "td,te->de", context_low, branch_low, preferred_element_type=jnp.float32
                ),
            ],
            axis=1,
        ).astype(jnp.bfloat16),
        "shard",
        scatter_dimension=0,
        tiled=True,
    )
    grad_input = jnp.einsum("te,de->td", query_low, w_query, preferred_element_type=jnp.float32)
    grad_input = grad_input + jnp.einsum(
        "te,de->td", key_low, w_key, preferred_element_type=jnp.float32
    )
    grad_input = grad_input + jnp.einsum(
        "te,de->td", value_low, w_value, preferred_element_type=jnp.float32
    )
    grad_tokens = (grad_input + d_first).astype(jnp.bfloat16)[None]
    vectors = jnp.stack(
        [
            jnp.sum(query_low.astype(jnp.float32), axis=0),
            jnp.sum(value_low.astype(jnp.float32), axis=0),
            jnp.sum(branch_low.astype(jnp.float32), axis=0),
            grad_gain_mid,
            grad_shift_mid,
            jnp.sum(feed_low.astype(jnp.float32), axis=0),
            grad_gain_end,
            grad_shift_end,
        ]
    )
    vector_part, up_bias_part = (
        lax.psum_scatter(
            vectors.astype(jnp.bfloat16), "shard", scatter_dimension=1, tiled=True
        ).astype(jnp.float32),
        lax.psum_scatter(
            jnp.sum(up_low.astype(jnp.float32), axis=0).astype(jnp.bfloat16),
            "shard",
            scatter_dimension=0,
            tiled=True,
        ).astype(jnp.float32),
    )
    mixer_total, up_total, down_total, vector_total, up_bias_total = (
        lax.psum(mixer_part, "rep").astype(jnp.float32),
        lax.psum(grad_up, "rep").astype(jnp.float32),
        lax.psum(grad_down, "rep").astype(jnp.float32),
        lax.psum(vector_part.astype(jnp.bfloat16), "rep").astype(jnp.float32),
        lax.psum(up_bias_part.astype(jnp.bfloat16), "rep").astype(jnp.float32),
    )
    return (
        output,
        grad_tokens,
        mixer_total[:, 0:D],
        mixer_total[:, D : 2 * D],
        mixer_total[:, 2 * D : 3 * D],
        vector_total[0],
        vector_total[1],
        mixer_total[:, 3 * D : 4 * D],
        vector_total[2],
        vector_total[3],
        vector_total[4],
        up_total,
        up_bias_total,
        down_total,
        vector_total[5],
        vector_total[6],
        vector_total[7],
    )


def solution(mesh):
    in_specs = (
        P("rep", "shard", None),
        P("rep", "shard"),
        P("rep", "shard"),
        P("shard", None),
        P("shard", None),
        P("shard", None),
        P("shard"),
        P("shard"),
        P("shard", None),
        P("shard"),
        P("shard"),
        P("shard"),
        P("shard", None),
        P("shard"),
        P("shard", None),
        P("shard"),
        P("shard"),
        P("shard"),
        P("rep", "shard", None),
    )
    out_specs = (
        P("rep", "shard", None),
        P("rep", "shard", None),
        P("shard", None),
        P("shard", None),
        P("shard", None),
        P("shard"),
        P("shard"),
        P("shard", None),
        P("shard"),
        P("shard"),
        P("shard"),
        P("shard", None),
        P("shard"),
        P("shard", None),
        P("shard"),
        P("shard"),
        P("shard"),
    )
    return jax.shard_map(shards, mesh=mesh, in_specs=in_specs, out_specs=out_specs, check_vma=False)
```

profile of v0, /device:TPU:0, one launch (start us, length us, event | category | flops | bytes accessed | tf_op | source)
XLA Modules:
  0.0 958.1 jit_solution(7064987100216604116)
XLA Ops:
  12.3 39.7 %all-gather.10.cloned.1.call-done = bf16[768,768]{1,0:T(8,128)(2,1)} async-done(((bf16[48,768]{1,0:T(8,128)(2,1)}), bf16[768,768]{1,0:T(8,128)(2,1)}) %all-gather.10.cloned.1.call-update) | async-done | bytes 1179664 | tf_op jit(solution)/shard_map/all_gather | solution.py:140
  58.3 59.9 %all-reduce.12 = (bf16[768]{0:T(1024)(128)(2,1)S(1)}, bf16[768]{0:T(1024)(128)(2,1)S(1)}, bf16[3072]{0:T(1024)(128)(2,1)S(1)}, bf16[768]{0:T(1024)(128)(2,1)S(1)...) all-reduce(bf16[768]{0:T(1024)(128)(2,1)S(1)} %dynamic-update-slice, ...), channel_id=1, replica_groups=mesh['rep'=2,'shard'=16] {'shard'}, use_global_device_ids=true, to_apply=%add.1 | all-reduce | flops 8448 | bytes 33792
  123.5 59.3 %all-reduce = s32[3072]{0:T(1024)S(1)} all-reduce(s32[3072]{0:T(1024)S(1)} %dynamic-update-slice), channel_id=2, replica_groups=mesh['rep'=2,'shard'=16] {'shard'}, use_global_device_ids=true, to_apply=%add | all-reduce | flops 3072 | bytes 24576
  187.3 15.0 %reshape.236 = bf16[6,512,12,64]{3,2,1,0:T(8,128)(2,1)} reshape(bf16[3072,768]{1,0:T(8,128)(2,1)} %all-gather.12.cloned.1.call-done) | data formatting | bytes 9437184 | tf_op jit(solution)/shard_map/reshape;reshape | solution.py:23
  202.3 13.6 %copy.64 = bf16[6,512,12,64]{1,3,2,0:T(8,128)(2,1)} copy(bf16[6,512,12,64]{3,2,1,0:T(8,128)(2,1)} %reshape.236) | data formatting | bytes 9437184
  215.9 25.9 %all-gather.18.cloned.1.call-done = bf16[3072,768]{1,0:T(8,128)(2,1)} async-done(((bf16[192,768]{1,0:T(8,128)(2,1)}), bf16[3072,768]{1,0:T(8,128)(2,1)}) %all-gather.18.cloned.1.call-update) | async-done | bytes 4718608 | tf_op jit(solution)/shard_map/all_gather | solution.py:172
  241.9 15.0 %reshape.237 = bf16[6,512,12,64]{3,2,1,0:T(8,128)(2,1)} reshape(bf16[3072,768]{1,0:T(8,128)(2,1)} %all-gather.18.cloned.1.call-done) | data formatting | bytes 9437184 | tf_op jit(solution)/shard_map/reshape;reshape | solution.py:23
  256.9 13.5 %copy.65 = bf16[6,512,12,64]{1,3,2,0:T(8,128)(2,1)} copy(bf16[6,512,12,64]{3,2,1,0:T(8,128)(2,1)} %reshape.237) | data formatting | bytes 9437184
  270.4 44.5 %while.28 = (s32[]{:T(128)}, f32[12,192]{1,0:T(8,128)S(1)}, f32[12,192]{1,0:T(8,128)S(1)}, f32[192,12,64]{0,2,1:T(8,128)S(1)}, s32[192]{0:T(256)S(1)}, /*index=5...) while((s32[]{:T(128)}, f32[12,192]{1,0:T(8,128)S(1)}, ...), condition=%wide.region_3.4_spmd.clone, body=%wide.region_0.3_spmd.clone.sunk | while | flops 317879808 | bytes 17750924 | solution.py:28
  317.9 18.6 %all-gather.22.cloned.1.call-done = bf16[768,3072]{1,0:T(8,128)(2,1)} async-done(((bf16[48,3072]{1,0:T(8,128)(2,1)}), bf16[768,3072]{1,0:T(8,128)(2,1)}) %all-gather.22.cloned.1.call-update) | async-done | bytes 4718608 | tf_op jit(solution)/shard_map/all_gather | solution.py:150
  336.5 8.9 fusion.49
  345.4 45.6 %all-gather.24.cloned.1.call-done = bf16[3072,768]{1,0:T(8,128)(2,1)} async-done(((bf16[192,768]{1,0:T(8,128)(2,1)}), bf16[3072,768]{1,0:T(8,128)(2,1)}) %all-gather.24.cloned.1.call-update) | async-done | bytes 4718608 | tf_op jit(solution)/shard_map/all_gather | solution.py:152
  391.0 4.0 fusion.101
  405.6 79.0 %while.29 = (s32[]{:T(128)}, f32[192,12,64]{0,2,1:T(8,128)S(1)}, bf16[6,512,1536]{2,1,0:T(8,128)(2,1)}, bf16[6,512,12,64]{1,3,2,0:T(8,128)(2,1)}, s32[192]{0:T(2...) while((s32[]{:T(128)}, f32[192,12,64]{0,2,1:T(8,128)S(1)}, ...), condition=%wide.region_14.15_spmd.clone, body=%wide.region_13.14_spmd.clone.sunk | while | flops 771244032 | bytes 44384276 | solution.py:35
  487.6 106.9 %reduce-scatter.10.cloned.1.call-done = bf16[192,1536]{1,0:T(8,128)(2,1)} async-done(((bf16[3072,1536]{1,0:T(8,128)(2,1)}), bf16[192,1536]{1,0:T(8,128)(2,1)}) %reduce-scatter.10.cloned.1.call-update) | async-done | bytes 589840 | tf_op jit(solution)/shard_map/reduce_scatter | solution.py:277
  600.1 6.6 copy.74
  608.1 3.7 convolution_convert_fusion.1
  621.5 33.9 %all-reduce.11 = (bf16[768]{0:T(1024)(128)(2,1)S(1)}, bf16[3072]{0:T(1024)(128)(2,1)S(1)}) all-reduce(bf16[768]{0:T(1024)(128)(2,1)S(1)} %dynamic-update-slice.9, bf16[3072]{0:T(1024)(128)(2,1)} %get-tuple-element.398), channel_id=1, replica_groups=mesh['rep'=2,'shard'=16] {'shard'}, use_global_device_ids=true, to_apply=%add.9 | all-reduce | flops 3840 | bytes 15360
  656.1 26.6 %reduce-scatter.16.cloned.1.call-done = bf16[48,3072]{1,0:T(8,128)(2,1)} async-done(((bf16[768,3072]{1,0:T(8,128)(2,1)}), bf16[48,3072]{1,0:T(8,128)(2,1)}) %reduce-scatter.16.cloned.1.call-update) | async-done | bytes 294928
  684.8 76.5 %reduce-scatter.12.cloned.1.call-done = bf16[48,3072]{1,0:T(8,128)(2,1)} async-done(((bf16[768,3072]{1,0:T(8,128)(2,1)}), bf16[48,3072]{1,0:T(8,128)(2,1)}) %reduce-scatter.12.cloned.1.call-update) | async-done | bytes 294928 | tf_op jit(solution)/shard_map/reduce_scatter | solution.py:227
  761.3 78.5 %reduce-scatter.14.cloned.1.call-done = bf16[192,768]{1,0:T(8,128)(2,1)} async-done(((bf16[3072,768]{1,0:T(8,128)(2,1)}), bf16[192,768]{1,0:T(8,128)(2,1)}) %reduce-scatter.14.cloned.1.call-update) | async-done | bytes 294928 | tf_op jit(solution)/shard_map/reduce_scatter | solution.py:217
  843.9 52.0 %reduce-scatter.18.cloned.1.call-done = bf16[48,8]{1,0:T(8,128)(2,1)} async-done(((bf16[768,8]{1,0:T(8,128)(2,1)}), bf16[48,8]{1,0:T(8,128)(2,1)}) %reduce-scatter.18.cloned.1.call-update) | async-done | bytes 784
  896.7 4.9 all-reduce.13
  902.7 41.9 %all-reduce.17.cloned.1.call-done = (bf16[48,3072]{0,1:T(8,128)(2,1)}, bf16[48,3072]{1,0:T(8,128)(2,1)}, bf16[192,768]{1,0:T(8,128)(2,1)}) async-done(((bf16[48,3072]{0,1:T(8,128)(2,1)}, bf16[48,3072]{1,0:T(8,128)(2,1)}, bf16[192,768]{1,0:T(8,128)(2,1)}), (bf16[48,3072]{0,1:T(8,128)(2,1)}, bf16[48,3072]{1,0:T(8,128)(2,1)}, bf16[192,768]{1,0:T(8,128)(2,1)})) %all-reduce.17.cloned.1.call-update) | async-done | bytes 884752 | tf_op jit(solution)/shard_map/psum | solution.py:333
  (418 shorter events, 189.8 us)
Async XLA Ops:
  7.2 111.0 %copy-start.2 = (bf16[1,192,768]{2,1,0:T(8,128)(2,1)S(1)}, bf16[1,192,768]{2,1,0:T(8,128)(2,1)}, u32[]{:S(2)}) copy-start(bf16[1,192,768]{2,1,0:T(8,128)(2,1)} %param.23) | copy-start | bytes 884740
  7.3 44.7 %all-gather.10.cloned.1.call-start = ((), (), s32[]{:S(2)}) async-start(), calls=%async_computation.5 | async-start | bytes 1253376 | tf_op jit(solution)/shard_map/all_gather | solution.py:140
  9.0 109.2 %all-gather.16.cloned.1.call-start = ((), (), s32[]{:S(2)}) async-start(), calls=%async_computation.8 | async-start | bytes 1253376 | tf_op jit(solution)/shard_map/all_gather | solution.py:141
  10.6 110.1 %copy-start.30 = (f32[48,768]{1,0:T(8,128)S(1)}, f32[48,768]{1,0:T(8,128)}, u32[]{:S(2)}) copy-start(f32[48,768]{1,0:T(8,128)} %param.31) | copy-start | bytes 442372
  10.6 172.8 %all-gather.14.cloned.1.call-start = ((), (), s32[]{:S(2)}) async-start(), calls=%async_computation.7 | async-start | bytes 1253376 | tf_op jit(solution)/shard_map/all_gather | solution.py:139
  12.2 109.2 %copy-start.28 = (f32[48,3072]{1,0:T(8,128)S(1)}, f32[48,3072]{1,0:T(8,128)}, u32[]{:S(2)}) copy-start(f32[48,3072]{1,0:T(8,128)} %param.35) | copy-start | bytes 1769476
  12.2 175.1 %all-gather.12.cloned.1.call-start = ((), (), s32[]{:S(2)}) async-start(), calls=%async_computation.6 | async-start | bytes 5013504 | tf_op jit(solution)/shard_map/all_gather | solution.py:171
  54.5 187.3 %all-gather.18.cloned.1.call-start = ((), (), s32[]{:S(2)}) async-start(), calls=%async_computation.9 | async-start | bytes 5013504 | tf_op jit(solution)/shard_map/all_gather | solution.py:172
  120.7 194.4 %all-gather.20.cloned.1.call-start = ((), (), s32[]{:S(2)}) async-start(), calls=%async_computation.10 | async-start | bytes 1253376 | tf_op jit(solution)/shard_map/all_gather | solution.py:142
  121.4 215.1 %all-gather.22.cloned.1.call-start = ((), (), s32[]{:S(2)}) async-start(), calls=%async_computation.11 | async-start | bytes 5013504 | tf_op jit(solution)/shard_map/all_gather | solution.py:150
  122.2 268.8 %all-gather.24.cloned.1.call-start = ((), (), s32[]{:S(2)}) async-start(), calls=%async_computation.12 | async-start | bytes 5013504 | tf_op jit(solution)/shard_map/all_gather | solution.py:152
  123.0 471.5 %reduce-scatter.10.cloned.1.call-start = ((), (), s32[]{:S(2)}) async-start(), calls=%async_computation.13 | async-start | bytes 10027008 | tf_op jit(solution)/shard_map/reduce_scatter | solution.py:277
  317.0 85.4 %copy-start.4 = (f32[192,768]{1,0:T(8,128)}, f32[192,768]{1,0:T(8,128)S(1)}, u32[]{:S(2)}) copy-start(f32[192,768]{1,0:T(8,128)S(1)} %get-tuple-element.393) | copy-start | bytes 1769476
  317.0 85.4 %copy-start.31 = (f32[192]{0:T(256)}, f32[192]{0:T(256)S(1)}, u32[]{:S(2)}) copy-start(f32[192]{0:T(256)S(1)} %broadcast_multiply_fusion.5) | copy-start | bytes 2308
  317.3 85.2 %copy-start.35 = (f32[192]{0:T(256)}, f32[192]{0:T(256)S(1)}, u32[]{:S(2)}) copy-start(f32[192]{0:T(256)S(1)} %add_rsqrt_fusion.1) | copy-start | bytes 2308
  484.6 198.0 %reduce-scatter.16.cloned.1.call-start = ((), (), s32[]{:S(2)}) async-start(), calls=%async_computation.16 | async-start | bytes 5013504
  606.7 154.6 %reduce-scatter.12.cloned.1.call-start = ((), (), s32[]{:S(2)}) async-start(), calls=%async_computation.14 | async-start | bytes 5013504 | tf_op jit(solution)/shard_map/reduce_scatter | solution.py:227
  611.9 227.9 %reduce-scatter.14.cloned.1.call-start = ((), (), s32[]{:S(2)}) async-start(), calls=%async_computation.15 | async-start | bytes 5013504 | tf_op jit(solution)/shard_map/reduce_scatter | solution.py:217
  617.0 278.9 %reduce-scatter.18.cloned.1.call-start = ((), (), s32[]{:S(2)}) async-start(), calls=%async_computation.17 | async-start | bytes 208896
  620.1 219.8 %copy-start.7 = (f32[192,768]{1,0:T(8,128)S(1)}, f32[192,768]{1,0:T(8,128)}, u32[]{:S(2)}) copy-start(f32[192,768]{1,0:T(8,128)} %copy-done.6) | copy-start | bytes 1769476
  620.1 219.8 %copy-start.34 = (f32[192]{0:T(256)S(1)}, f32[192]{0:T(256)}, u32[]{:S(2)}) copy-start(f32[192]{0:T(256)} %copy-done.33) | copy-start | bytes 2308
  620.1 219.8 %copy-start.38 = (f32[192]{0:T(256)S(1)}, f32[192]{0:T(256)}, u32[]{:S(2)}) copy-start(f32[192]{0:T(256)} %copy-done.37) | copy-start | bytes 2308
  620.1 324.5 %all-reduce.17.cloned.1.call-start = ((), (), s32[]{:S(2)}) async-start(), calls=%async_computation.18 | async-start | bytes 2752512 | tf_op jit(solution)/shard_map/psum | solution.py:333
  621.5 219.2 %copy-start.23 = (f32[192,768]{1,0:T(8,128)S(1)}, f32[192,768]{1,0:T(8,128)}, u32[]{:S(2)}) copy-start(f32[192,768]{1,0:T(8,128)} %fusion.103) | copy-start | bytes 1769476
  (72 other events, 740.1 us)
Sparse Core Ops, SparseCore 0:
  11.0 41.0 all-gather.9
  54.9 37.3 all-gather.15
  95.1 37.1 all-gather.13
  135.0 52.2 all-gather.11
  190.0 51.7 all-gather.17
  244.6 36.8 all-gather.19
  284.3 52.0 all-gather.21
  339.3 51.6 all-gather.23
  484.7 109.7 reduce-scatter.9
  606.8 75.7 reduce-scatter.15
  686.5 74.7 reduce-scatter.11
  765.0 74.7 reduce-scatter.13
  843.3 52.5 reduce-scatter.17
  898.2 46.3 all-reduce.16
where the time goes:
time: 963 us; the launch traced here: 958 us
  waiting for transfers between devices  515 us (53%)
  blocking collectives  158 us (16%)
  matrix products  130 us (13%)
  local copies, waits for them, and re-layouts  106 us (11%)
  other arithmetic  31.2 us (3%)
  between operations  16.8 us (2%)
    unnamed x3, blocking collectives  153 us
    reduce_scatter x1, waiting for transfers between devices, shards(): lax.psum_scatter(key_value_terms.astype(jnp.bfloat16), 'shard', scatter_d...  107 us
    unnamed x16, waiting for transfers between devices  78.8 us
    reduce_scatter x1, waiting for transfers between devices, shards(): lax.psum_scatter(jnp.einsum('tf,td->fd', active_low, feed_low, preferred_...  78.5 us
    reduce_scatter x1, waiting for transfers between devices, shards(): lax.psum_scatter(jnp.einsum('td,tf->df', middle_low, up_low, preferred_el...  76.5 us
    unnamed x148, local copies, waits for them, and re-layouts  49.1 us
    all_gather x1, waiting for transfers between devices, shards(): lax.all_gather(down_weight.astype(jnp.bfloat16), 'shard', axis=0, tiled=T...  45.6 us
    psum x1, waiting for transfers between devices, shards(): lax.psum(mixer_part, 'rep').astype(jnp.float32)  41.9 us
  transfers between devices with their start and end apart: 14, of which 11 were waited for; matrix products, arithmetic and copies ran while one was open for 16% of the time, Pallas kernels for 0%

commit v1 on v0

--- a/solution.py
+++ b/solution.py
@@ -2,6 +2,7 @@
 import jax.numpy as jnp
 from jax import lax
 from jax.sharding import PartitionSpec as P
+from jax.lax import all_gather
 
 D = 768
 HEADS = 12
@@ -329,8 +330,12 @@
             tiled=True,
         ).astype(jnp.float32),
     )
+
+    def _reach_space(z, mesh_dim="rep"):
+        return jnp.sum(all_gather(z, mesh_dim), axis=0)
+
     mixer_total, up_total, down_total, vector_total, up_bias_total = (
-        lax.psum(mixer_part, "rep").astype(jnp.float32),
+        _reach_space(mixer_part).astype(jnp.float32),
         lax.psum(grad_up, "rep").astype(jnp.float32),
         lax.psum(grad_down, "rep").astype(jnp.float32),
         lax.psum(vector_part.astype(jnp.bfloat16), "rep").astype(jnp.float32),

time: 963 us -> 859 us (0.89)
  waiting for transfers between devices: 515 us -> 412 us
    reduce_scatter x1, waiting for transfers between devices: 76.5 us -> 0.01 us  [shards(): lax.psum_scatter(jnp.einsum('td,tf->df', middle_low, up_low, preferred_el...]
    reduce_scatter x0 -> x1, waiting for transfers between devices: none -> 71.5 us  [shards(): lax.psum_scatter(jnp.concatenate([jnp.einsum('td,te->de', own_tokens, que...]
    unnamed x16 -> x15, waiting for transfers between devices: 78.8 us -> 31.2 us
    psum x1, waiting for transfers between devices: 41.9 us -> 0.01 us  [shards(): lax.psum(grad_up, 'rep').astype(jnp.float32)]
    reduce_scatter x1, waiting for transfers between devices: 78.5 us -> 61.3 us  [shards(): lax.psum_scatter(jnp.einsum('tf,td->fd', active_low, feed_low, preferred_...]
    unnamed x148 -> x151, local copies, waits for them, and re-layouts: 49.1 us -> 42.9 us
  transfers between devices with their start and end apart: 14 -> 14, of which waited for: 11 -> 9; matrix products, arithmetic and copies ran while one was open for 16% -> 27% of each run, Pallas kernels for 0% -> 0%
where the time goes in v1:
time: 859 us; the launch traced here: 855 us
  waiting for transfers between devices  412 us (48%)
  blocking collectives  165 us (19%)
  matrix products  129 us (15%)
  local copies, waits for them, and re-layouts  97.2 us (11%)
  other arithmetic  33 us (4%)
  between operations  16.9 us (2%)
    unnamed x3, blocking collectives  152 us
    reduce_scatter x1, waiting for transfers between devices, shards(): lax.psum_scatter(key_value_terms.astype(jnp.bfloat16), 'shard', scatter_d...  111 us
    reduce_scatter x1, waiting for transfers between devices, shards(): lax.psum_scatter(jnp.concatenate([jnp.einsum('td,te->de', own_tokens, que...  71.5 us
    reduce_scatter x1, waiting for transfers between devices, shards(): lax.psum_scatter(jnp.einsum('tf,td->fd', active_low, feed_low, preferred_...  61.3 us
    all_gather x1, waiting for transfers between devices, shards(): lax.all_gather(down_weight.astype(jnp.bfloat16), 'shard', axis=0, tiled=T...  45.9 us
    unnamed x151, local copies, waits for them, and re-layouts  42.9 us
    all_gather x1, waiting for transfers between devices, shards(): lax.all_gather(key_weight.astype(jnp.bfloat16), 'shard', axis=0, tiled=True)  39.7 us
    unnamed x15, waiting for transfers between devices  31.2 us
  transfers between devices with their start and end apart: 14, of which 9 were waited for; matrix products, arithmetic and copies ran while one was open for 27% of the time, Pallas kernels for 0%

profile of v1, /device:TPU:0, one launch (start us, length us, event | category | flops | bytes accessed | tf_op | source)
XLA Modules:
  0.0 855.1 jit_solution(9248638300299919688)
XLA Ops:
  12.3 39.7 %all-gather.11.cloned.1.call-done = bf16[768,768]{1,0:T(8,128)(2,1)} async-done(((bf16[48,768]{1,0:T(8,128)(2,1)}), bf16[768,768]{1,0:T(8,128)(2,1)}) %all-gather.11.cloned.1.call-update) | async-done | bytes 1179664 | tf_op jit(solution)/shard_map/all_gather | solution.py:141
  58.3 59.9 %all-reduce.12 = (bf16[3072]{0:T(1024)(128)(2,1)S(1)}, bf16[768]{0:T(1024)(128)(2,1)S(1)}, bf16[768]{0:T(1024)(128)(2,1)S(1)}, bf16[768]{0:T(1024)(128)(2,1)S(1)...) all-reduce(bf16[3072]{0:T(1024)(128)(2,1)S(1)} %dynamic-update-slic, ...), channel_id=1, replica_groups=mesh['rep'=2,'shard'=16] {'shard'}, use_global_device_ids=true, to_apply=%add.6 | all-reduce | flops 8448 | bytes 33792
  123.5 59.3 %all-reduce = s32[3072]{0:T(1024)S(1)} all-reduce(s32[3072]{0:T(1024)S(1)} %dynamic-update-slice), channel_id=2, replica_groups=mesh['rep'=2,'shard'=16] {'shard'}, use_global_device_ids=true, to_apply=%add | all-reduce | flops 3072 | bytes 24576
  187.3 15.1 %reshape.237 = bf16[6,512,12,64]{3,2,1,0:T(8,128)(2,1)} reshape(bf16[3072,768]{1,0:T(8,128)(2,1)} %all-gather.13.cloned.1.call-done) | data formatting | bytes 9437184 | tf_op jit(solution)/shard_map/reshape;reshape | solution.py:24
  202.4 13.5 %copy.57 = bf16[6,512,12,64]{1,3,2,0:T(8,128)(2,1)} copy(bf16[6,512,12,64]{3,2,1,0:T(8,128)(2,1)} %reshape.237) | data formatting | bytes 9437184
  215.9 25.9 %all-gather.19.cloned.1.call-done = bf16[3072,768]{1,0:T(8,128)(2,1)} async-done(((bf16[192,768]{1,0:T(8,128)(2,1)}), bf16[3072,768]{1,0:T(8,128)(2,1)}) %all-gather.19.cloned.1.call-update) | async-done | bytes 4718608 | tf_op jit(solution)/shard_map/all_gather | solution.py:173
  241.9 15.1 %reshape.238 = bf16[6,512,12,64]{3,2,1,0:T(8,128)(2,1)} reshape(bf16[3072,768]{1,0:T(8,128)(2,1)} %all-gather.19.cloned.1.call-done) | data formatting | bytes 9437184 | tf_op jit(solution)/shard_map/reshape;reshape | solution.py:24
  256.9 13.5 %copy.58 = bf16[6,512,12,64]{1,3,2,0:T(8,128)(2,1)} copy(bf16[6,512,12,64]{3,2,1,0:T(8,128)(2,1)} %reshape.238) | data formatting | bytes 9437184
  270.5 40.2 %while.28 = (s32[]{:T(128)}, f32[12,192]{1,0:T(8,128)S(1)}, f32[12,192]{1,0:T(8,128)S(1)}, f32[192,12,64]{0,2,1:T(8,128)S(1)}, s32[192]{0:T(256)S(1)}, /*index=5...) while((s32[]{:T(128)}, f32[12,192]{1,0:T(8,128)S(1)}, ...), condition=%wide.region_3.4_spmd.clone, body=%wide.region_0.3_spmd.clone.sunk | while | flops 317879808 | bytes 17750924 | solution.py:29
  313.7 22.7 %all-gather.23.cloned.1.call-done = bf16[768,3072]{1,0:T(8,128)(2,1)} async-done(((bf16[48,3072]{1,0:T(8,128)(2,1)}), bf16[768,3072]{1,0:T(8,128)(2,1)}) %all-gather.23.cloned.1.call-update) | async-done | bytes 4718608 | tf_op jit(solution)/shard_map/all_gather | solution.py:151
  336.3 8.6 %fusion.49 = (bf16[192,3072]{1,0:T(8,128)(2,1)S(1)}, f32[192,3072]{1,0:T(8,128)}) fusion(f32[3072]{0:T(1024)S(1)} %convert_element_type.218, bf16[768,3072]{1,0:T(8,128)(2,1)} %all-gather.23.cloned.1.call-done, f32[192,768]{1,0:T(8,128)S(1)} %get-tuple-element.341, f32[768]{0:T(1024)S(1)} %convert_element_type.214, f32[768]{0:T(1024)S(1)} %convert_element_type.212, ...), kind=kOutput, calls=%fused_computation.66 | convolution fusion | flops 945635328 | bytes 8867328 | tf_op jit(solution)/shard_map/dot_general | solution.py:202
  345.0 45.9 %all-gather.25.cloned.1.call-done = bf16[3072,768]{1,0:T(8,128)(2,1)} async-done(((bf16[192,768]{1,0:T(8,128)(2,1)}), bf16[3072,768]{1,0:T(8,128)(2,1)}) %all-gather.25.cloned.1.call-update) | async-done | bytes 4718608 | tf_op jit(solution)/shard_map/all_gather | solution.py:153
  390.9 3.7 fusion.101
  401.3 3.7 convolution_convert_fusion.1
  405.1 5.2 multiply_reduce_fusion.1
  420.1 75.1 %while.29 = (s32[]{:T(128)}, f32[192,12,64]{0,2,1:T(8,128)S(1)}, bf16[6,512,1536]{2,1,0:T(8,128)(2,1)}, bf16[6,512,12,64]{1,3,2,0:T(8,128)(2,1)}, s32[192]{0:T(2...) while((s32[]{:T(128)}, f32[192,12,64]{0,2,1:T(8,128)S(1)}, ...), condition=%wide.region_14.15_spmd.clone, body=%wide.region_13.14_spmd.clone.sunk | while | flops 771244032 | bytes 44517508 | solution.py:36
  496.6 61.3 %reduce-scatter.14.cloned.1.call-done = bf16[192,768]{1,0:T(8,128)(2,1)} async-done(((bf16[3072,768]{1,0:T(8,128)(2,1)}), bf16[192,768]{1,0:T(8,128)(2,1)}) %reduce-scatter.14.cloned.1.call-update) | async-done | bytes 294928 | tf_op jit(solution)/shard_map/reduce_scatter | solution.py:218
  561.0 111.5 %reduce-scatter.10.cloned.1.call-done = bf16[192,1536]{1,0:T(8,128)(2,1)} async-done(((bf16[3072,1536]{1,0:T(8,128)(2,1)}), bf16[192,1536]{1,0:T(8,128)(2,1)}) %reduce-scatter.10.cloned.1.call-update) | async-done | bytes 589840 | tf_op jit(solution)/shard_map/reduce_scatter | solution.py:278
  679.4 6.6 copy.64
  687.6 32.6 %all-reduce.11 = (bf16[768]{0:T(1024)(128)(2,1)S(1)}, bf16[3072]{0:T(1024)(128)(2,1)S(1)}) all-reduce(bf16[768]{0:T(1024)(128)(2,1)S(1)} %dynamic-update-slice.9, bf16[3072]{0:T(1024)(128)(2,1)S(1)} %copy-done.52), channel_id=1, replica_groups=mesh['rep'=2,'shard'=16] {'shard'}, use_global_device_ids=true, to_apply=%add.9 | all-reduce | flops 3840 | bytes 15360
  730.4 31.0 %reduce-scatter.18.cloned.1.call-done = bf16[48,8]{1,0:T(8,128)(2,1)} async-done(((bf16[768,8]{1,0:T(8,128)(2,1)}), bf16[48,8]{1,0:T(8,128)(2,1)}) %reduce-scatter.18.cloned.1.call-update) | async-done | bytes 784
  762.1 4.9 all-reduce.13
  768.1 71.5 %reduce-scatter.16.cloned.1.call-done = bf16[48,3072]{1,0:T(8,128)(2,1)} async-done(((bf16[768,3072]{1,0:T(8,128)(2,1)}), bf16[48,3072]{1,0:T(8,128)(2,1)}) %reduce-scatter.16.cloned.1.call-update) | async-done | bytes 294928 | tf_op jit(solution)/shard_map/reduce_scatter | solution.py:286
  839.6 7.9 all-gather.1
  (470 shorter events, 177.8 us)
Async XLA Ops:
  7.2 111.0 %copy-start.2 = (bf16[1,192,768]{2,1,0:T(8,128)(2,1)S(1)}, bf16[1,192,768]{2,1,0:T(8,128)(2,1)}, u32[]{:S(2)}) copy-start(bf16[1,192,768]{2,1,0:T(8,128)(2,1)} %param.23) | copy-start | bytes 884740
  7.3 44.7 %all-gather.11.cloned.1.call-start = ((), (), s32[]{:S(2)}) async-start(), calls=%async_computation.5 | async-start | bytes 1253376 | tf_op jit(solution)/shard_map/all_gather | solution.py:141
  9.0 109.2 %all-gather.17.cloned.1.call-start = ((), (), s32[]{:S(2)}) async-start(), calls=%async_computation.8 | async-start | bytes 1253376 | tf_op jit(solution)/shard_map/all_gather | solution.py:142
  10.6 110.1 %copy-start.31 = (f32[48,768]{1,0:T(8,128)S(1)}, f32[48,768]{1,0:T(8,128)}, u32[]{:S(2)}) copy-start(f32[48,768]{1,0:T(8,128)} %param.31) | copy-start | bytes 442372
  10.6 172.2 %all-gather.15.cloned.1.call-start = ((), (), s32[]{:S(2)}) async-start(), calls=%async_computation.7 | async-start | bytes 1253376 | tf_op jit(solution)/shard_map/all_gather | solution.py:140
  12.2 109.2 %copy-start.24 = (f32[48,3072]{1,0:T(8,128)S(1)}, f32[48,3072]{1,0:T(8,128)}, u32[]{:S(2)}) copy-start(f32[48,3072]{1,0:T(8,128)} %param.35) | copy-start | bytes 1769476
  12.2 175.1 %all-gather.13.cloned.1.call-start = ((), (), s32[]{:S(2)}) async-start(), calls=%async_computation.6 | async-start | bytes 5013504 | tf_op jit(solution)/shard_map/all_gather | solution.py:172
  54.5 67.8 %copy-start.25 = (f32[192,768]{1,0:T(8,128)S(1)}, f32[192,768]{1,0:T(8,128)}, u32[]{:S(2)}) copy-start(f32[192,768]{1,0:T(8,128)} %param.37) | copy-start | bytes 1769476
  54.5 187.3 %all-gather.19.cloned.1.call-start = ((), (), s32[]{:S(2)}) async-start(), calls=%async_computation.9 | async-start | bytes 5013504 | tf_op jit(solution)/shard_map/all_gather | solution.py:173
  120.7 190.8 %all-gather.21.cloned.1.call-start = ((), (), s32[]{:S(2)}) async-start(), calls=%async_computation.10 | async-start | bytes 1253376 | tf_op jit(solution)/shard_map/all_gather | solution.py:143
  121.4 215.0 %all-gather.23.cloned.1.call-start = ((), (), s32[]{:S(2)}) async-start(), calls=%async_computation.11 | async-start | bytes 5013504 | tf_op jit(solution)/shard_map/all_gather | solution.py:151
  122.2 268.7 %all-gather.25.cloned.1.call-start = ((), (), s32[]{:S(2)}) async-start(), calls=%async_computation.12 | async-start | bytes 5013504 | tf_op jit(solution)/shard_map/all_gather | solution.py:153
  123.0 373.6 %reduce-scatter.12.cloned.1.call-start = ((), (), s32[]{:S(2)}) async-start(), calls=%async_computation.14 | async-start | bytes 5013504 | tf_op jit(solution)/shard_map/reduce_scatter | solution.py:228
  123.1 267.8 %copy-start.26 = (f32[768]{0:T(1024)}, f32[768]{0:T(1024)S(1)}, u32[]{:S(2)}) copy-start(f32[768]{0:T(1024)S(1)} %convert_element_type.212) | copy-start | bytes 9220
  123.1 267.8 %copy-start.32 = (f32[768]{0:T(1024)}, f32[768]{0:T(1024)S(1)}, u32[]{:S(2)}) copy-start(f32[768]{0:T(1024)S(1)} %convert_element_type.214) | copy-start | bytes 9220
  123.2 271.7 %copy-start.35 = (f32[768]{0:T(1024)}, f32[768]{0:T(1024)S(1)}, u32[]{:S(2)}) copy-start(f32[768]{0:T(1024)S(1)} %convert_element_type.224) | copy-start | bytes 9220
  313.4 86.8 %copy-start.37 = (f32[192]{0:T(256)}, f32[192]{0:T(256)S(1)}, u32[]{:S(2)}) copy-start(f32[192]{0:T(256)S(1)} %broadcast_multiply_fusion.5) | copy-start | bytes 2308
  313.7 86.6 %copy-start.43 = (f32[192]{0:T(256)}, f32[192]{0:T(256)S(1)}, u32[]{:S(2)}) copy-start(f32[192]{0:T(256)S(1)} %add_rsqrt_fusion.1) | copy-start | bytes 2308
  405.0 152.9 %reduce-scatter.14.cloned.1.call-start = ((), (), s32[]{:S(2)}) async-start(), calls=%async_computation.15 | async-start | bytes 5013504 | tf_op jit(solution)/shard_map/reduce_scatter | solution.py:218
  419.5 253.0 %reduce-scatter.10.cloned.1.call-start = ((), (), s32[]{:S(2)}) async-start(), calls=%async_computation.13 | async-start | bytes 10027008 | tf_op jit(solution)/shard_map/reduce_scatter | solution.py:278
  495.3 228.5 %all-reduce.17.cloned.1.call-start = ((), (), s32[]{:S(2)}) async-start(), calls=%async_computation.18 | async-start | bytes 1179648 | tf_op jit(solution)/shard_map/psum | solution.py:339
  496.5 64.5 %copy-start.14 = (bf16[192,12,64]{0,2,1:T(8,128)(2,1)}, bf16[192,12,64]{0,2,1:T(8,128)(2,1)S(1)}, u32[]{:S(2)}) copy-start(bf16[192,12,64]{0,2,1:T(8,128)(2,1)S(1)} %get-tuple-element.323) | copy-start | bytes 884740
  557.9 203.4 %reduce-scatter.18.cloned.1.call-start = ((), (), s32[]{:S(2)}) async-start(), calls=%async_computation.17 | async-start | bytes 208896
  674.5 165.2 %reduce-scatter.16.cloned.1.call-start = ((), (), s32[]{:S(2)}) async-start(), calls=%async_computation.16 | async-start | bytes 5013504 | tf_op jit(solution)/shard_map/reduce_scatter | solution.py:286
  (100 other events, 999.9 us)
Sparse Core Ops, SparseCore 0:
  11.0 41.0 all-gather.10
  54.9 37.3 all-gather.16
  95.1 37.1 all-gather.14
  135.0 52.2 all-gather.12
  190.0 51.8 all-gather.18
  244.6 36.8 all-gather.20
  284.3 51.9 all-gather.22
  339.2 51.6 all-gather.24
  405.2 74.1 reduce-scatter.11
  483.0 74.8 reduce-scatter.13
  562.0 110.4 reduce-scatter.9
  674.7 29.6 all-reduce.16
  707.9 53.3 reduce-scatter.17
  765.0 74.5 reduce-scatter.15
